TPU v7x, 32 devices: a whole 2x2x4 slice. The times are simulated.
32 devices in a mesh: node: 4 (over y, core), rep: 8 (over z, x).
Axes of the slice: x: 2, y: 2, z: 4, core: 2. Of those that a mesh axis runs over, the one named last changes fastest.
Arguments:
- tokens: bfloat16 [8192, 2048], P(('node', 'rep')), may hold values from -60 to 60
- cotangent: bfloat16 [8192, 512], P(('node', 'rep')), may hold values from -6 to 6
- value_weight: bfloat16 [2048, 512], P('node'), may hold values from -0.25 to 0.25
Outputs:
- input_grad: bfloat16 [8192, 2048], P(('node', 'rep'))
- update: float32 [2048, 512], P('node')
All inputs are finite; a program needn't handle non-finite values.
Results may differ from a plain program's by a relative error of at most 0.025.
Values may be sent and summed in bfloat16 or wider, within the bound.
A program may use at most 64 MiB of HBM per device.

v0:
```python
import math
import jax
import jax.numpy as jnp
from jax import lax
from jax.sharding import PartitionSpec as P

DIN = 2048
HD = 128
NS_ITERS = 5
coef_a = 3.4445
coef_b = -4.775
coef_c = 2.0315
epsilon = 1e-07


def per_device(tokens, cotangent, value_weight):
    width = value_weight.shape[1]
    local_rows = value_weight.shape[0]
    heads = width // HD
    input_grad = lax.dot_general(
        cotangent,
        lax.all_gather(value_weight, "node", axis=0, tiled=True),
        (((1,), (1,)), ((), ())),
        preferred_element_type=jnp.float32,
    ).astype(jnp.bfloat16)
    partial_rows = lax.psum_scatter(
        lax.dot_general(
            tokens, cotangent, (((0,), (0,)), ((), ())), preferred_element_type=jnp.float32
        ).astype(jnp.bfloat16),
        "node",
        scatter_dimension=0,
        tiled=True,
    ).astype(jnp.float32)
    gradient = lax.psum(partial_rows, "rep")
    blocks = gradient.reshape(local_rows, heads, HD)
    local_raw = jnp.einsum("rhi,rhj->hij", blocks, blocks, precision=lax.Precision.HIGHEST)
    gram_raw = lax.psum(local_raw, "node")
    squares = jnp.einsum("hii->h", gram_raw)
    divisor = jnp.sqrt(squares) + epsilon
    start_iterate = blocks / divisor[None, :, None]
    gram = gram_raw / (divisor * divisor)[:, None, None]
    identity = jnp.broadcast_to(jnp.eye(HD, dtype=jnp.float32), (heads, HD, HD))
    total = identity
    for step in range(NS_ITERS):
        factor = (
            coef_a * identity
            + coef_b * gram
            + coef_c * jnp.einsum("hij,hjk->hik", gram, gram, precision=lax.Precision.HIGHEST)
        )
        total = jnp.einsum("hij,hjk->hik", total, factor, precision=lax.Precision.HIGHEST)
        if step + 1 < NS_ITERS:
            halfway = jnp.einsum("hij,hjk->hik", gram, factor, precision=lax.Precision.HIGHEST)
            gram = jnp.einsum("hji,hjk->hik", factor, halfway, precision=lax.Precision.HIGHEST)
    iterate = jnp.einsum("rhi,hij->rhj", start_iterate, total, precision=lax.Precision.HIGHEST)
    update = 0.2 * math.sqrt(DIN) * iterate.reshape(local_rows, width)
    return (input_grad, update)


def solution(mesh):
    in_specs = (P(("node", "rep"), None), P(("node", "rep"), None), P("node", None))
    out_specs = (P(("node", "rep"), None), P("node", None))
    return jax.shard_map(
        per_device, mesh=mesh, in_specs=in_specs, out_specs=out_specs, check_vma=False
    )
```

profile of v0, /device:TPU:0, one launch (start us, length us, event | category | flops | bytes accessed | tf_op | source)
XLA Modules:
  0.0 206.4 jit_solution(13655678280055105823)
XLA Ops:
  7.2 1.2 copy-done
  8.4 3.0 %convolution_convert_fusion = bf16[2048,512]{1,0:T(8,128)(2,1)} fusion(bf16[256,2048]{1,0:T(8,128)(2,1)S(1)} %copy-done, bf16[256,512]{1,0:T(8,128)(2,1)} %param.4), kind=kOutput, calls=%fused_computation | convolution fusion | flops 537919488 | bytes 3407872 | tf_op jit(solution)/shard_map/dot_general | solution.py:27
  11.5 34.0 %reduce-scatter.2.cloned.1.call-done = bf16[512,512]{1,0:T(8,128)(2,1)} async-done(((bf16[2048,512]{1,0:T(8,128)(2,1)}), bf16[512,512]{1,0:T(8,128)(2,1)}) %reduce-scatter.2.cloned.1.call-update) | async-done | bytes 524304 | tf_op jit(solution)/shard_map/reduce_scatter | solution.py:26
  45.5 2.1 %copy_bitcast_fusion = f32[512,4,128]{2,0,1:T(8,128)} fusion(bf16[512,512]{1,0:T(8,128)(2,1)} %reduce-scatter.2.cloned.1.call-done), kind=kLoop, calls=%fused_computation.13 | loop fusion | flops 262144 | bytes 1572864 | tf_op jit(solution)/shard_map/reshape | solution.py:35
  47.7 0.7 all-gather.2.cloned.1.call-update
  48.5 79.5 %all-reduce.3.cloned.1.call-done = f32[512,4,128]{2,0,1:T(8,128)} async-done(((f32[512,4,128]{2,0,1:T(8,128)}), f32[512,4,128]{2,0,1:T(8,128)}) %all-reduce.3.cloned.1.call-update) | async-done | bytes 1048592 | tf_op jit(solution)/shard_map/psum | solution.py:34
  128.0 4.1 %fusion.13 = f32[4,128,128]{2,1,0:T(8,128)} fusion(f32[512,4,128]{2,0,1:T(8,128)} %all-reduce.3.cloned.1.call-done), kind=kOutput, calls=%fused_computation.28 | convolution fusion | flops 402653184 | bytes 1310720 | tf_op jit(solution)/shard_map/rhi,rhj->hij/dot_general | solution.py:36
  132.1 19.6 %all-gather.2.cloned.1.call-done = bf16[2048,512]{1,0:T(8,128)(2,1)} async-done(((bf16[512,512]{1,0:T(8,128)(2,1)}), bf16[2048,512]{1,0:T(8,128)(2,1)}) %all-gather.2.cloned.1.call-update) | async-done | bytes 2097168 | tf_op jit(solution)/shard_map/all_gather | solution.py:22
  151.8 3.3 %convolution_convert_fusion.1 = bf16[256,2048]{1,0:T(8,128)(2,1)} fusion(bf16[256,512]{1,0:T(8,128)(2,1)S(1)} %copy-done.2, bf16[2048,512]{1,0:T(8,128)(2,1)} %all-gather.2.cloned.1.call-done), kind=kOutput, calls=%fused_computation.1 | convolution fusion | flops 537395200 | bytes 3407872 | tf_op jit(solution)/shard_map/dot_general | solution.py:20
  155.1 31.8 %all-reduce.5.cloned.1.call-done = f32[4,128,128]{2,1,0:T(8,128)} async-done(((f32[4,128,128]{2,1,0:T(8,128)}), f32[4,128,128]{2,1,0:T(8,128)}) %all-reduce.5.cloned.1.call-update) | async-done | bytes 262160 | tf_op jit(solution)/shard_map/psum | solution.py:37
  186.8 1.2 select_reduce_fusion
  188.0 1.6 fusion.4
  190.0 0.4 fusion.11
  190.5 0.6 fusion.14
  191.4 0.4 fusion.16
  191.8 0.4 fusion.15
  192.2 0.6 fusion.17
  194.0 0.6 fusion.20
  195.0 0.4 fusion.22
  195.4 0.4 fusion.21
  195.9 0.6 fusion.23
  196.8 0.6 fusion.24
  197.5 1.1 convolution_multiply_fusion
  198.5 1.3 copy.11
  (25 shorter events, 2.9 us)
Async XLA Ops:
  7.2 1.2 copy-start
  7.2 38.4 %reduce-scatter.2.cloned.1.call-start = ((), (), s32[]{:S(2)}) async-start(), calls=%async_computation.2 | async-start | bytes 2621440 | tf_op jit(solution)/shard_map/reduce_scatter | solution.py:26
  11.5 116.6 %all-reduce.3.cloned.1.call-start = ((), (), s32[]{:S(2)}) async-start(), calls=%async_computation.3 | async-start | bytes 2097152 | tf_op jit(solution)/shard_map/psum | solution.py:34
  47.6 104.2 %copy-start.2 = (bf16[256,512]{1,0:T(8,128)(2,1)S(1)}, bf16[256,512]{1,0:T(8,128)(2,1)}, u32[]{:S(2)}) copy-start(bf16[256,512]{1,0:T(8,128)(2,1)} %param.4) | copy-start | bytes 786436
  47.6 104.1 %all-gather.2.cloned.1.call-start = ((), (), s32[]{:S(2)}) async-start(), calls=%async_computation.1 | async-start | bytes 2621440 | tf_op jit(solution)/shard_map/all_gather | solution.py:22
  48.4 138.5 %all-reduce.5.cloned.1.call-start = ((), (), s32[]{:S(2)}) async-start(), calls=%async_computation.4 | async-start | bytes 524288 | tf_op jit(solution)/shard_map/psum | solution.py:37
  186.8 3.2 %copy-start.3 = (f32[4,128,128]{2,1,0:T(8,128)S(1)}, f32[4,128,128]{2,1,0:T(8,128)}, u32[]{:S(2)}) copy-start(f32[4,128,128]{2,1,0:T(8,128)} %all-reduce.5.cloned.1.call-done) | copy-start | bytes 786436
  195.0 2.4 %copy-start.1 = (f32[512,4,128]{2,0,1:T(8,128)S(1)}, f32[512,4,128]{2,0,1:T(8,128)}, u32[]{:S(2)}) copy-start(f32[512,4,128]{2,0,1:T(8,128)} %all-reduce.3.cloned.1.call-done) | copy-start | bytes 3145732
Sparse Core Ops, SparseCore 0:
  11.6 33.9 reduce-scatter.1
  49.6 78.3 all-reduce.2
  129.6 22.1 all-gather.1
  154.5 32.2 all-reduce.4
where the time goes:
time: 207 us; the launch traced here: 206 us
  waiting for transfers between devices  166 us (80%)
  matrix products  20.8 us (10%)
  between operations  14 us (7%)
  other arithmetic  3.28 us (2%)
  local copies, waits for them, and re-layouts  2.5 us (1%)
    psum x1, waiting for transfers between devices, per_device(): gradient = lax.psum(partial_rows, 'rep')  79.5 us
    reduce_scatter x1, waiting for transfers between devices, per_device(): lax.psum_scatter(lax.dot_general(tokens, cotangent, (((0,), (0,)), ((), (...  34 us
    psum x1, waiting for transfers between devices, per_device(): gram_raw = lax.psum(local_raw, 'node')  31.8 us
    all_gather x1, waiting for transfers between devices, per_device(): lax.all_gather(value_weight, 'node', axis=0, tiled=True)  19.6 us
  transfers between devices with their start and end apart: 4, of which 4 were waited for; matrix products, arithmetic and copies ran while one was open for 4% of the time, Pallas kernels for 0%

commit v1 on v0

--- a/solution.py
+++ b/solution.py
@@ -11,6 +11,15 @@
 coef_b = -4.775
 coef_c = 2.0315
 epsilon = 1e-07
+
+
+def add_in_pairs(block, axis):
+    size = lax.axis_size(axis)
+    total, far = (block, 1)
+    while far < size:
+        total = total + lax.ppermute(total, axis, [(i, i ^ far) for i in range(size)])
+        far = 2 * far
+    return total
 
 
 def per_device(tokens, cotangent, value_weight):
@@ -34,7 +43,7 @@
     gradient = lax.psum(partial_rows, "rep")
     blocks = gradient.reshape(local_rows, heads, HD)
     local_raw = jnp.einsum("rhi,rhj->hij", blocks, blocks, precision=lax.Precision.HIGHEST)
-    gram_raw = lax.psum(local_raw, "node")
+    gram_raw = add_in_pairs(local_raw, "node")
     squares = jnp.einsum("hii->h", gram_raw)
     divisor = jnp.sqrt(squares) + epsilon
     start_iterate = blocks / divisor[None, :, None]

time: 207 us -> 175 us (0.85)
  waiting for transfers between devices: 166 us -> 135 us
    psum x1 -> x0, waiting for transfers between devices: 31.8 us -> none  [per_device(): gram_raw = lax.psum(local_raw, 'node')]
  transfers between devices with their start and end apart: 4 -> 5, of which waited for: 4 -> 4; matrix products, arithmetic and copies ran while one was open for 4% -> 4% of each run, Pallas kernels for 0% -> 0%
where the time goes in v1:
time: 175 us
  waiting for transfers between devices  135 us (77%)
  matrix products  18.9 us (11%)
  between operations  14 us (8%)
  local copies, waits for them, and re-layouts  2.49 us (1%)
  other arithmetic  2.3 us (1%)
    psum x1, waiting for transfers between devices, per_device(): gradient = lax.psum(partial_rows, 'rep')  79.6 us
    reduce_scatter x1, waiting for transfers between devices, per_device(): lax.psum_scatter(lax.dot_general(tokens, cotangent, (((0,), (0,)), ((), (...  34 us
    all_gather x1, waiting for transfers between devices, per_device(): lax.all_gather(value_weight, 'node', axis=0, tiled=True)  19.6 us
  transfers between devices with their start and end apart: 5, of which 4 were waited for; matrix products, arithmetic and copies ran while one was open for 4% of the time, Pallas kernels for 0%

profile of v1, /device:TPU:0, one launch (start us, length us, event | category | flops | bytes accessed | tf_op | source)
XLA Modules:
  0.0 174.9 jit_solution(6550995823562379731)
XLA Ops:
  7.2 1.2 copy-done
  8.4 3.0 %convolution_convert_fusion = bf16[2048,512]{1,0:T(8,128)(2,1)} fusion(bf16[256,2048]{1,0:T(8,128)(2,1)S(1)} %copy-done, bf16[256,512]{1,0:T(8,128)(2,1)} %param.4), kind=kOutput, calls=%fused_computation | convolution fusion | flops 537919488 | bytes 3407872 | tf_op jit(solution)/shard_map/dot_general | solution.py:36
  11.5 34.0 %reduce-scatter.2.cloned.1.call-done = bf16[512,512]{1,0:T(8,128)(2,1)} async-done(((bf16[2048,512]{1,0:T(8,128)(2,1)}), bf16[512,512]{1,0:T(8,128)(2,1)}) %reduce-scatter.2.cloned.1.call-update) | async-done | bytes 524304 | tf_op jit(solution)/shard_map/reduce_scatter | solution.py:35
  45.5 2.1 %copy_bitcast_fusion = f32[512,4,128]{2,0,1:T(8,128)} fusion(bf16[512,512]{1,0:T(8,128)(2,1)} %reduce-scatter.2.cloned.1.call-done), kind=kLoop, calls=%fused_computation.12 | loop fusion | flops 262144 | bytes 1572864 | tf_op jit(solution)/shard_map/reshape | solution.py:44
  47.7 0.7 all-gather.2.cloned.1.call-update
  48.4 79.6 %all-reduce.2.cloned.1.call-done = f32[512,4,128]{2,0,1:T(8,128)} async-done(((f32[512,4,128]{2,0,1:T(8,128)}), f32[512,4,128]{2,0,1:T(8,128)}) %all-reduce.2.cloned.1.call-update) | async-done | bytes 1048592 | tf_op jit(solution)/shard_map/psum | solution.py:43
  128.0 3.4 %fusion.12 = f32[4,128,128]{2,1,0:T(8,128)S(1)} fusion(f32[512,4,128]{2,0,1:T(8,128)} %all-reduce.2.cloned.1.call-done), kind=kOutput, calls=%fused_computation.28 | convolution fusion | flops 402653184 | bytes 1310720 | tf_op jit(solution)/shard_map/rhi,rhj->hij/dot_general | solution.py:45
  131.5 1.5 collective-permute-done
  133.0 1.5 collective-permute-start.1
  134.6 19.6 %all-gather.2.cloned.1.call-done = bf16[2048,512]{1,0:T(8,128)(2,1)} async-done(((bf16[512,512]{1,0:T(8,128)(2,1)}), bf16[2048,512]{1,0:T(8,128)(2,1)}) %all-gather.2.cloned.1.call-update) | async-done | bytes 2097168 | tf_op jit(solution)/shard_map/all_gather | solution.py:31
  154.2 3.3 %convolution_convert_fusion.1 = bf16[256,2048]{1,0:T(8,128)(2,1)} fusion(bf16[256,512]{1,0:T(8,128)(2,1)S(1)} %copy-done.2, bf16[2048,512]{1,0:T(8,128)(2,1)} %all-gather.2.cloned.1.call-done), kind=kOutput, calls=%fused_computation.1 | convolution fusion | flops 537395200 | bytes 3407872 | tf_op jit(solution)/shard_map/dot_general | solution.py:29
  157.7 0.5 add_add_fusion
  158.1 0.4 fusion.10
  159.0 0.6 fusion.13
  160.0 0.4 fusion.15
  160.4 0.4 fusion.14
  160.8 0.6 fusion.16
  161.8 0.4 fusion.18
  162.2 0.4 fusion.17
  162.6 0.6 fusion.19
  164.4 0.6 fusion.22
  165.4 0.6 fusion.23
  166.0 1.1 convolution_multiply_fusion
  167.1 1.3 copy.11
  (25 shorter events, 3.1 us)
Async XLA Ops:
  7.2 1.2 copy-start
  7.2 38.4 %reduce-scatter.2.cloned.1.call-start = ((), (), s32[]{:S(2)}) async-start(), calls=%async_computation.2 | async-start | bytes 2621440 | tf_op jit(solution)/shard_map/reduce_scatter | solution.py:35
  11.5 116.6 %all-reduce.2.cloned.1.call-start = ((), (), s32[]{:S(2)}) async-start(), calls=%async_computation.3 | async-start | bytes 2097152 | tf_op jit(solution)/shard_map/psum | solution.py:43
  47.6 106.6 %copy-start.2 = (bf16[256,512]{1,0:T(8,128)(2,1)S(1)}, bf16[256,512]{1,0:T(8,128)(2,1)}, u32[]{:S(2)}) copy-start(bf16[256,512]{1,0:T(8,128)(2,1)} %param.4) | copy-start | bytes 786436
  47.7 106.5 %all-gather.2.cloned.1.call-start = ((), (), s32[]{:S(2)}) async-start(), calls=%async_computation.1 | async-start | bytes 2621440 | tf_op jit(solution)/shard_map/all_gather | solution.py:31
  131.4 1.6 collective-permute-start
  133.0 24.5 %collective-permute-start.1 = (f32[4,128,128]{2,1,0:T(8,128)S(1)}, f32[4,128,128]{2,1,0:T(8,128)S(1)}, u32[]{:S(2)}, u32[]{:S(2)}) collective-permute-start(f32[4,128,128]{2,1,0:T(8,128)S(1)} %add.51), channel_id=1, source_target_pairs={{0,16},{8,24},{16,0},{24,8},{1,17},{9,25},{17,1},{25,9},{2,18},{10... | collective-permute-start | bytes 786440 | tf_op jit(solution)/shard_map/ppermute | solution.py:20
  163.6 2.4 %copy-start.1 = (f32[512,4,128]{2,0,1:T(8,128)S(1)}, f32[512,4,128]{2,0,1:T(8,128)}, u32[]{:S(2)}) copy-start(f32[512,4,128]{2,0,1:T(8,128)} %all-reduce.2.cloned.1.call-done) | copy-start | bytes 3145732
Sparse Core Ops, SparseCore 0:
  11.6 33.9 reduce-scatter.1
  49.6 78.3 all-reduce.1
  129.6 24.5 all-gather.1

commit v2 on v0

--- a/solution.py
+++ b/solution.py
@@ -11,6 +11,14 @@
 coef_b = -4.775
 coef_c = 2.0315
 epsilon = 1e-07
+
+
+def added_up(block, mesh_axis):
+    size, total = (lax.axis_size(mesh_axis), block)
+    for stride in [1 << k for k in range(size.bit_length() - 1)]:
+        pairs = [(i, i ^ stride) for i in range(size)]
+        total = total + lax.ppermute(total, mesh_axis, pairs)
+    return total
 
 
 def per_device(tokens, cotangent, value_weight):
@@ -31,7 +39,7 @@
         scatter_dimension=0,
         tiled=True,
     ).astype(jnp.float32)
-    gradient = lax.psum(partial_rows, "rep")
+    gradient = added_up(partial_rows, "rep")
     blocks = gradient.reshape(local_rows, heads, HD)
     local_raw = jnp.einsum("rhi,rhj->hij", blocks, blocks, precision=lax.Precision.HIGHEST)
     gram_raw = lax.psum(local_raw, "node")

time: 207 us -> 201 us (0.971)
  waiting for transfers between devices: 166 us -> 153 us
  starting transfers between devices: 0.16 us -> 5.72 us
    ppermute x0 -> x3, waiting for transfers between devices: none -> 89.5 us  [added_up(): total = total + lax.ppermute(total, mesh_axis, pairs)]
    psum x1 -> x0, waiting for transfers between devices: 79.5 us -> none  [per_device(): gradient = lax.psum(partial_rows, 'rep')]
    all_gather x1, waiting for transfers between devices: 19.6 us -> 0.02 us  [per_device(): lax.all_gather(value_weight, 'node', axis=0, tiled=True)]
    ppermute x0 -> x3, starting transfers between devices: none -> 5.59 us  [added_up(): total = total + lax.ppermute(total, mesh_axis, pairs)]
    psum x1, waiting for transfers between devices: 31.8 us -> 29.1 us  [per_device(): gram_raw = lax.psum(local_raw, 'node')]
    reshape x1 -> x0, other arithmetic: 2.08 us -> none  [per_device(): blocks = gradient.reshape(local_rows, heads, HD)]
  transfers between devices with their start and end apart: 4 -> 6, of which waited for: 4 -> 5; matrix products, arithmetic and copies ran while one was open for 4% -> 4% of each run, Pallas kernels for 0% -> 0%
where the time goes in v2:
time: 201 us
  waiting for transfers between devices  153 us (76%)
  matrix products  20.4 us (10%)
  between operations  14 us (7%)
  starting transfers between devices  5.72 us (3%)
  other arithmetic  4.02 us (2%)
  local copies, waits for them, and re-layouts  3.72 us (2%)
    ppermute x3, waiting for transfers between devices, added_up(): total = total + lax.ppermute(total, mesh_axis, pairs)  89.5 us
    reduce_scatter x1, waiting for transfers between devices, per_device(): lax.psum_scatter(lax.dot_general(tokens, cotangent, (((0,), (0,)), ((), (...  34 us
    psum x1, waiting for transfers between devices, per_device(): gram_raw = lax.psum(local_raw, 'node')  29.1 us
    ppermute x3, starting transfers between devices, added_up(): total = total + lax.ppermute(total, mesh_axis, pairs)  5.59 us
  transfers between devices with their start and end apart: 6, of which 5 were waited for; matrix products, arithmetic and copies ran while one was open for 4% of the time, Pallas kernels for 0%

profile of v2, /device:TPU:0, one launch (start us, length us, event | category | flops | bytes accessed | tf_op | source)
XLA Modules:
  0.0 200.6 jit_solution(69287042591062721)
XLA Ops:
  7.2 1.2 copy-done
  8.4 3.0 %convolution_convert_fusion = bf16[2048,512]{1,0:T(8,128)(2,1)} fusion(bf16[256,2048]{1,0:T(8,128)(2,1)S(1)} %copy-done, bf16[256,512]{1,0:T(8,128)(2,1)} %param.4), kind=kOutput, calls=%fused_computation | convolution fusion | flops 537919488 | bytes 3407872 | tf_op jit(solution)/shard_map/dot_general | solution.py:35
  11.5 34.0 %reduce-scatter.2.cloned.1.call-done = bf16[512,512]{1,0:T(8,128)(2,1)} async-done(((bf16[2048,512]{1,0:T(8,128)(2,1)}), bf16[512,512]{1,0:T(8,128)(2,1)}) %reduce-scatter.2.cloned.1.call-update) | async-done | bytes 524304 | tf_op jit(solution)/shard_map/reduce_scatter | solution.py:34
  45.5 1.2 convert_element_type.15
  46.8 1.5 collective-permute-start
  48.4 23.3 %collective-permute-done = f32[512,512]{1,0:T(8,128)} collective-permute-done((f32[512,512]{1,0:T(8,128)S(1)}, f32[512,512]{1,0:T(8,128)}, u32[]{:S(2)}, u32[]{:S(2)}) %collective-permute-start) | collective-permute-done | bytes 1048608 | tf_op jit(solution)/shard_map/ppermute | solution.py:20
  71.7 1.4 convert_add_fusion
  73.1 1.6 collective-permute-start.1
  74.6 22.4 %collective-permute-done.1 = f32[512,512]{1,0:T(8,128)S(1)} collective-permute-done((f32[512,512]{1,0:T(8,128)S(1)}, f32[512,512]{1,0:T(8,128)S(1)}, u32[]{:S(2)}, u32[]{:S(2)}) %collective-permute-start.1) | collective-permute-done | bytes 1048608 | tf_op jit(solution)/shard_map/ppermute | solution.py:20
  97.2 2.5 %collective-permute-start.2 = (f32[512,512]{1,0:T(8,128)S(1)}, f32[512,512]{1,0:T(8,128)S(1)}, u32[]{:S(2)}, u32[]{:S(2)}) collective-permute-start(f32[512,512]{1,0:T(8,128)S(1)} %add.55), channel_id=1, source_target_pairs={{0,4},{1,5},{2,6},{3,7},{4,0},{5,1},{6,2},{7,3},{8,12},{9,13},{10,... | collective-permute-start | bytes 3145736 | tf_op jit(solution)/shard_map/ppermute | solution.py:20
  99.8 43.9 %collective-permute-done.2 = f32[512,512]{1,0:T(8,128)S(1)} collective-permute-done((f32[512,512]{1,0:T(8,128)S(1)}, f32[512,512]{1,0:T(8,128)S(1)}, u32[]{:S(2)}, u32[]{:S(2)}) %collective-permute-start.2) | collective-permute-done | bytes 1048608 | tf_op jit(solution)/shard_map/ppermute | solution.py:20
  143.6 2.7 %fusion.5 = f32[4,128,128]{2,1,0:T(8,128)} fusion(f32[512,512]{1,0:T(8,128)S(1)} %add.55, f32[512,512]{1,0:T(8,128)S(1)} %collective-permute-done.2), kind=kOutput, calls=%fused_computation.14 | convolution fusion | flops 402915328 | bytes 2359296 | tf_op jit(solution)/shard_map/rhi,rhj->hij/dot_general | solution.py:44
  146.4 3.3 %convolution_convert_fusion.1 = bf16[256,2048]{1,0:T(8,128)(2,1)} fusion(bf16[256,512]{1,0:T(8,128)(2,1)S(1)} %copy-done.2, bf16[2048,512]{1,0:T(8,128)(2,1)} %all-gather.2.cloned.1.call-done), kind=kOutput, calls=%fused_computation.1 | convolution fusion | flops 537395200 | bytes 3407872 | tf_op jit(solution)/shard_map/dot_general | solution.py:28
  149.7 29.1 %all-reduce.2.cloned.1.call-done = f32[4,128,128]{2,1,0:T(8,128)} async-done(((f32[4,128,128]{2,1,0:T(8,128)}), f32[4,128,128]{2,1,0:T(8,128)}) %all-reduce.2.cloned.1.call-update) | async-done | bytes 262160 | tf_op jit(solution)/shard_map/psum | solution.py:45
  178.8 1.2 select_reduce_fusion
  180.0 1.6 fusion.4
  181.6 0.4 fusion.14
  182.0 0.6 fusion.16
  183.4 0.6 fusion.19
  184.8 0.6 fusion.22
  186.2 0.6 fusion.25
  188.8 0.6 fusion.26
  189.4 2.1 %convolution_multiply_fusion = f32[4,128,512]{2,1,0:T(8,128)} fusion(f32[4,128,128]{1,2,0:T(8,128)S(1)} %fusion.26, f32[4]{0:T(128)S(1)} %get-tuple-element.4, f32[512,512]{1,0:T(8,128)S(1)} %add.55, f32[512,512]{1,0:T(8,128)S(1)} %collective-permute-done.2), kind=kOutput, calls=%fused_computation.2 | convolution fusion | flops 403439616 | bytes 3407888 | tf_op jit(solution)/shard_map/rhi,hij->rhj/dot_general | solution.py:62
  191.5 2.5 %copy.12 = f32[512,512]{1,0:T(8,128)} copy(f32[512,512]{0,1:T(8,128)} %bitcast.51) | data formatting | bytes 2097152
  (30 shorter events, 4.7 us)
Async XLA Ops:
  7.2 1.2 copy-start
  7.2 38.4 %reduce-scatter.2.cloned.1.call-start = ((), (), s32[]{:S(2)}) async-start(), calls=%async_computation.2 | async-start | bytes 2621440 | tf_op jit(solution)/shard_map/reduce_scatter | solution.py:34
  11.5 134.9 %all-gather.2.cloned.1.call-start = ((), (), s32[]{:S(2)}) async-start(), calls=%async_computation.1 | async-start | bytes 2621440 | tf_op jit(solution)/shard_map/all_gather | solution.py:30
  45.5 26.1 %copy-start.1 = (bf16[512,512]{1,0:T(8,128)(2,1)S(1)}, bf16[512,512]{1,0:T(8,128)(2,1)}, u32[]{:S(2)}) copy-start(bf16[512,512]{1,0:T(8,128)(2,1)} %reduce-scatter.2.cloned.1.call-done) | copy-start | bytes 1572868
  46.8 24.9 %collective-permute-start = (f32[512,512]{1,0:T(8,128)S(1)}, f32[512,512]{1,0:T(8,128)}, u32[]{:S(2)}, u32[]{:S(2)}) collective-permute-start(f32[512,512]{1,0:T(8,128)S(1)} %convert_element_type.15), channel_id=1, source_target_pairs={{0,1},{1,0},{2,3},{3,2},{4,5},{5,4},{6,7},{7,6},{8,9},{9,8},{10,11... | collective-permute-start | bytes 3145736 | tf_op jit(solution)/shard_map/ppermute | solution.py:20
  48.3 130.5 %all-reduce.2.cloned.1.call-start = ((), (), s32[]{:S(2)}) async-start(), calls=%async_computation.3 | async-start | bytes 524288 | tf_op jit(solution)/shard_map/psum | solution.py:45
  73.1 23.9 %collective-permute-start.1 = (f32[512,512]{1,0:T(8,128)S(1)}, f32[512,512]{1,0:T(8,128)S(1)}, u32[]{:S(2)}, u32[]{:S(2)}) collective-permute-start(f32[512,512]{1,0:T(8,128)S(1)} %convert_add_fusion), channel_id=1, source_target_pairs={{0,2},{1,3},{2,0},{3,1},{4,6},{5,7},{6,4},{7,5},{8,10},{9,11},{10,... | collective-permute-start | bytes 3145736 | tf_op jit(solution)/shard_map/ppermute | solution.py:20
  97.2 49.2 %copy-start.2 = (bf16[256,512]{1,0:T(8,128)(2,1)S(1)}, bf16[256,512]{1,0:T(8,128)(2,1)}, u32[]{:S(2)}) copy-start(bf16[256,512]{1,0:T(8,128)(2,1)} %param.4) | copy-start | bytes 786436
  97.2 46.4 %collective-permute-start.2 = (f32[512,512]{1,0:T(8,128)S(1)}, f32[512,512]{1,0:T(8,128)S(1)}, u32[]{:S(2)}, u32[]{:S(2)}) collective-permute-start(f32[512,512]{1,0:T(8,128)S(1)} %add.55), channel_id=1, source_target_pairs={{0,4},{1,5},{2,6},{3,7},{4,0},{5,1},{6,2},{7,3},{8,12},{9,13},{10,... | collective-permute-start | bytes 3145736 | tf_op jit(solution)/shard_map/ppermute | solution.py:20
  178.8 2.8 %copy-start.3 = (f32[4,128,128]{2,1,0:T(8,128)S(1)}, f32[4,128,128]{2,1,0:T(8,128)}, u32[]{:S(2)}) copy-start(f32[4,128,128]{2,1,0:T(8,128)} %all-reduce.2.cloned.1.call-done) | copy-start | bytes 786436
Sparse Core Ops, SparseCore 0:
  11.6 33.9 reduce-scatter.1
  48.4 21.6 all-gather.1
  146.5 32.2 all-reduce.1
